TPU v7x, 256 devices: a whole 4x4x8 slice. The times are simulated.
256 devices in a mesh: gx: 16 (over z_hi, x, core), ev: 16 (over y, z_lo).
Axes of the slice: x: 4, y: 4, z: 8 (z_hi: 2, z_lo: 4; z = z_hi * 4 + z_lo), core: 2. Of those that a mesh axis runs over, the one named last changes fastest.
Arguments:
- partial_kernels: bfloat16 [16, 2048, 2, 8, 2048], P('ev', 'gx'), may hold values from -8 to 8
- illumination: float32 [2048, 8, 2048], P('gx', None, 'ev'), may hold values from 0.3 to 3
- classes_x: int32 [8, 2048], P(None, 'ev'), may hold values from 0 to 2
- classes_y: int32 [2048, 8], P('gx'), may hold values from 0 to 2
- widths_x: float32 [3], replicated, may hold values from 0.5 to 1
- widths_y: float32 [3], replicated, may hold values from 0.5 to 1
Outputs:
- conditioned: bfloat16 [2048, 2, 8, 2048], P('gx', None, None, 'ev')
All inputs are finite; a program needn't handle non-finite values.
Results may differ from a plain program's by a relative error of at most 0.0035.
Values may be sent and summed in bfloat16 or wider, within the bound.
A program may use at most 192 MiB of HBM per device.

v0:
```python
import jax
import jax.numpy as jnp
from jax import lax
from jax.sharding import PartitionSpec as P

BAND = 128


blend_weight = 0.25
soft_bound = 2.0


def with_halo(shard, sides, width):
    for axis, dim in sides:
        size, length = (lax.axis_size(axis), shard.shape[dim])
        up = [(i, (i + 1) % size) for i in range(size - 1)]
        down = [(j, i) for i, j in up]
        last = lax.slice_in_dim(shard, length - width, length, axis=dim)
        initial = lax.slice_in_dim(shard, 0, width, axis=dim)
        before = lax.ppermute(last, axis, up)
        after = lax.ppermute(initial, axis, down)
        shard = jnp.concatenate([before, shard, after], axis=dim)
    return shard


def smoother_window(length, fraction, first_row, rows, cols):
    row_pos = first_row + jnp.arange(rows, dtype=jnp.float32)
    col_pos = first_row - BAND + jnp.arange(cols, dtype=jnp.float32)
    offset = row_pos[:, None] - col_pos[None, :]
    inside = (jnp.abs(offset) <= BAND) & (col_pos[None, :] >= 0.0) & (col_pos[None, :] < length)
    distance = offset / (fraction * BAND)
    gaussian = jnp.where(inside, jnp.exp(-0.5 * distance * distance), jnp.float32(0.0))
    gaussian = gaussian / jnp.sum(gaussian, axis=1, keepdims=True)
    diagonal = jnp.where(offset == 0.0, jnp.float32(blend_weight), jnp.float32(0.0))
    return (gaussian + diagonal).astype(jnp.bfloat16)


def smooth_columns(columns, labels, matrices):
    summed = jnp.zeros((matrices[0].shape[0], columns.shape[1]), jnp.float32)
    for level in range(len(matrices)):
        product = jnp.dot(matrices[level], columns, preferred_element_type=jnp.float32)
        summed = summed + jnp.where(labels[None, :] == level, product, jnp.float32(0.0))
    return summed


def smooth_rows(row_block, labels, matrices):
    summed = jnp.zeros((row_block.shape[0], matrices[0].shape[0]), jnp.float32)
    for level in range(len(matrices)):
        product = lax.dot_general(
            row_block, matrices[level], (((1,), (1,)), ((), ())), preferred_element_type=jnp.float32
        )
        summed = summed + jnp.where(labels[:, None] == level, product, jnp.float32(0.0))
    return summed


def per_device(partial_kernels, illumination, classes_x, classes_y, widths_x, widths_y):
    own_part = partial_kernels[0]
    slab_x, kernels, planes, full_y = own_part.shape
    groups = lax.axis_size("ev")
    owners = lax.axis_size("gx")
    slab_y = full_y // groups
    full_x = slab_x * owners
    count_levels = widths_x.shape[0]
    pieces = own_part.reshape(slab_x, kernels, planes, groups, slab_y)
    arrived = lax.all_to_all(pieces, "ev", split_axis=3, concat_axis=3, tiled=True)
    summed = jnp.sum(arrived.astype(jnp.float32), axis=3)
    scaled = (summed / illumination[:, None, :, :]).astype(jnp.bfloat16)
    widened_x = with_halo(scaled, (("gx", 0),), BAND)
    first_x = (lax.axis_index("gx") * slab_x).astype(jnp.float32)
    windows_x = [
        smoother_window(full_x, widths_x[level], first_x, slab_x, slab_x + 2 * BAND)
        for level in range(count_levels)
    ]
    labels_x = jnp.broadcast_to(classes_x[None, :, :], (kernels, planes, slab_y)).reshape(-1)
    smoothed_x = smooth_columns(widened_x.reshape(slab_x + 2 * BAND, -1), labels_x, windows_x)
    bounded = (
        (soft_bound * jnp.tanh(smoothed_x / soft_bound))
        .astype(jnp.bfloat16)
        .reshape(slab_x, kernels, planes, slab_y)
    )
    widened_y = with_halo(bounded, (("ev", 3),), BAND)
    first_y = (lax.axis_index("ev") * slab_y).astype(jnp.float32)
    windows_y = [
        smoother_window(full_y, widths_y[level], first_y, slab_y, slab_y + 2 * BAND)
        for level in range(count_levels)
    ]
    labels_y = jnp.broadcast_to(classes_y[:, None, :], (slab_x, kernels, planes)).reshape(-1)
    smoothed_y = smooth_rows(widened_y.reshape(-1, slab_y + 2 * BAND), labels_y, windows_y)
    conditioned = smoothed_y.astype(jnp.bfloat16).reshape(slab_x, kernels, planes, slab_y)
    return conditioned


def solution(mesh):
    return jax.shard_map(
        per_device,
        mesh=mesh,
        in_specs=(
            P("ev", "gx", None, None, None),
            P("gx", None, "ev"),
            P(None, "ev"),
            P("gx", None),
            P(),
            P(),
        ),
        out_specs=P("gx", None, None, "ev"),
        check_vma=False,
    )
```

profile of v0, /device:TPU:15, one launch (start us, length us, event | category | flops | bytes accessed | tf_op | source)
XLA Modules:
  0.0 271.5 jit_solution(18154667136522794893)
XLA Ops:
  0.0 12.5 %copy.22 = bf16[1,128,2,8,2048]{1,4,3,2,0:T(8,128)(2,1)} copy(bf16[1,128,2,8,2048]{4,3,2,1,0:T(8,128)(2,1)} %param.6) | data formatting | bytes 16777216 | tf_op args[0]
  12.5 12.7 %copy.23 = bf16[128,2,8,16,128]{4,2,1,0,3:T(8,128)(2,1)} copy(bf16[128,2,8,16,128]{0,4,3,2,1:T(8,128)(2,1)} %bitcast.28) | data formatting | bytes 16777216 | tf_op jit(solution)/shard_map/reshape;squeeze | solution.py:64
  25.2 8.6 %all-to-all-start = ((bf16[128,2,8,16,128]{4,2,1,0,3:T(8,128)(2,1)}), bf16[128,2,8,16,128]{4,2,1,0,3:T(8,128)(2,1)}, u32[]{:S(2)}, u32[]{:S(2)}) async-start(bf16[128,2,8,16,128]{4,2,1,0,3:T(8,128)(2,1)} %copy.23), calls=%async_computation | async-start | bytes 16777216 | tf_op jit(solution)/shard_map/all_to_all | solution.py:65
  33.8 0.6 fusion.115
  36.5 0.4 fusion.82
  36.9 181.7 %all-to-all-done = bf16[128,2,8,16,128]{4,2,1,0,3:T(8,128)(2,1)} async-done(((bf16[128,2,8,16,128]{4,2,1,0,3:T(8,128)(2,1)}), bf16[128,2,8,16,128]{4,2,1,0,3:T(8,128)(2,1)}, u32[]{:S(2)}, u32[]{:S(2)}) %all-to-all-start) | async-done | bytes 8388640 | tf_op jit(solution)/shard_map/all_to_all | solution.py:65
  218.6 4.7 %convert_reduce_fusion = f32[128,2,8,128]{3,2,1,0:T(8,128)S(1)} fusion(bf16[128,2,8,16,128]{4,2,1,0,3:T(8,128)(2,1)} %all-to-all-done), kind=kLoop, calls=%fused_computation | loop fusion | flops 8126464 | bytes 9437184 | tf_op jit(solution)/shard_map/reduce_sum | solution.py:66
  223.3 0.1 divide_convert_fusion
  223.5 7.3 %collective-permute-start = (bf16[128,2,8,128]{3,2,1,0:T(8,128)(2,1)S(1)}, bf16[128,2,8,128]{3,2,1,0:T(8,128)(2,1)S(1)}, u32[]{:S(2)}, u32[]{:S(2)}) collective-permute-start(bf16[128,2,8,128]{3,2,1,0:T(8,128)(2,1)S(1)} %divide_convert_fusion), channel_id=1, source_target_pairs={{0,16},{16,32},{32,48},{48,64},{64,80},{80,96},{96,112},{112,128},... | collective-permute-start | bytes 1572872 | tf_op jit(solution)/shard_map/ppermute | solution.py:20
  230.8 1.9 collective-permute-start.1
  232.7 0.6 fusion.116
  235.1 0.1 copy.24
  235.3 0.1 eq.116
  235.5 0.1 copy.25
  235.7 0.1 eq.119
  235.8 0.1 copy.21
  236.0 0.1 eq.102
  236.2 0.7 collective-permute-done
  236.9 10.6 %collective-permute-done.1 = bf16[128,2,8,128]{3,2,1,0:T(8,128)(2,1)S(1)} collective-permute-done((bf16[128,2,8,128]{3,2,1,0:T(8,128)(2,1)S(1)}, bf16[128,2,8,128]{3,2,1,0:T(8,128)(2,1)S(1)}, u32[]{:S(2)}, u32[]{:S(2)}) %collective-permute-start.1) | collective-permute-done | bytes 524320 | tf_op jit(solution)/shard_map/ppermute | solution.py:21
  247.5 0.2 pad_maximum_fusion
  247.6 0.6 convolution_select_fusion.4
  248.2 0.6 fusion
  248.8 0.7 fusion.8
  249.6 4.1 %collective-permute-start.2 = (bf16[128,2,8,128]{3,2,1,0:T(8,128)(2,1)S(1)}, bf16[128,2,8,128]{3,2,1,0:T(8,128)(2,1)S(1)}, u32[]{:S(2)}, u32[]{:S(2)}) collective-permute-start(bf16[128,2,8,128]{3,2,1,0:T(8,128)(2,1)S(1)} %bitcast.33), channel_id=1, source_target_pairs={{0,1},{1,2},{2,3},{3,4},{4,5},{5,6},{6,7},{7,8},{8,9},{9,10},{10,1... | collective-permute-start | bytes 1572872 | tf_op jit(solution)/shard_map/ppermute | solution.py:20
  253.7 3.9 %collective-permute-start.3 = (bf16[128,2,8,128]{3,2,1,0:T(8,128)(2,1)S(1)}, bf16[128,2,8,128]{3,2,1,0:T(8,128)(2,1)S(1)}, u32[]{:S(2)}, u32[]{:S(2)}) collective-permute-start(bf16[128,2,8,128]{3,2,1,0:T(8,128)(2,1)S(1)} %bitcast.34), channel_id=1, source_target_pairs={{1,0},{2,1},{3,2},{4,3},{5,4},{6,5},{7,6},{8,7},{9,8},{10,9},{11,1... | collective-permute-start | bytes 1572872 | tf_op jit(solution)/shard_map/ppermute | solution.py:21
  257.7 0.4 fusion.80
  258.0 0.2 concatenate.15
  258.3 5.5 %collective-permute-done.2 = bf16[128,2,8,128]{3,2,1,0:T(8,128)(2,1)S(1)} collective-permute-done((bf16[128,2,8,128]{3,2,1,0:T(8,128)(2,1)S(1)}, bf16[128,2,8,128]{3,2,1,0:T(8,128)(2,1)S(1)}, u32[]{:S(2)}, u32[]{:S(2)}) %collective-permute-start.2) | collective-permute-done | bytes 524320 | tf_op jit(solution)/shard_map/ppermute | solution.py:20
  263.7 4.7 %collective-permute-done.3 = bf16[128,2,8,128]{3,2,1,0:T(8,128)(2,1)S(1)} collective-permute-done((bf16[128,2,8,128]{3,2,1,0:T(8,128)(2,1)S(1)}, bf16[128,2,8,128]{3,2,1,0:T(8,128)(2,1)S(1)}, u32[]{:S(2)}, u32[]{:S(2)}) %collective-permute-start.3) | collective-permute-done | bytes 524320 | tf_op jit(solution)/shard_map/ppermute | solution.py:21
  268.4 0.7 convolution_select_fusion.1
  269.2 0.7 convolution_select_fusion
  269.9 1.6 fusion.7
  (24 shorter events, 0.4 us)
Async XLA Ops:
  25.2 8.6 %copy-start.1 = (f32[3]{0:T(128)S(1)}, f32[3]{0:T(128)}, u32[]{:S(2)}) copy-start(f32[3]{0:T(128)} %param.10) | copy-start | bytes 40
  25.2 11.6 %copy-start.3 = (s32[8,128]{1,0:T(8,128)S(1)}, s32[8,128]{1,0:T(8,128)}, u32[]{:S(2)}) copy-start(s32[8,128]{1,0:T(8,128)} %param.8) | copy-start | bytes 12292
  25.2 11.6 %copy-start.4 = (s32[128,8]{0,1:T(8,128)S(1)}, s32[128,8]{0,1:T(8,128)}, u32[]{:S(2)}) copy-start(s32[128,8]{0,1:T(8,128)} %param.9) | copy-start | bytes 12292
  25.2 193.4 %all-to-all-start = ((bf16[128,2,8,16,128]{4,2,1,0,3:T(8,128)(2,1)}), bf16[128,2,8,16,128]{4,2,1,0,3:T(8,128)(2,1)}, u32[]{:S(2)}, u32[]{:S(2)}) async-start(bf16[128,2,8,16,128]{4,2,1,0,3:T(8,128)(2,1)} %copy.23), calls=%async_computation | async-start | bytes 16777216 | tf_op jit(solution)/shard_map/all_to_all | solution.py:65
  36.9 186.4 %copy-start = (f32[128,8,128]{2,1,0:T(8,128)S(1)}, f32[128,8,128]{2,1,0:T(8,128)}, u32[]{:S(2)}) copy-start(f32[128,8,128]{2,1,0:T(8,128)} %param.7) | copy-start | bytes 1572868
  223.3 9.4 %copy-start.2 = (f32[3]{0:T(128)S(1)}, f32[3]{0:T(128)}, u32[]{:S(2)}) copy-start(f32[3]{0:T(128)} %param.11) | copy-start | bytes 40
  223.5 13.4 %collective-permute-start = (bf16[128,2,8,128]{3,2,1,0:T(8,128)(2,1)S(1)}, bf16[128,2,8,128]{3,2,1,0:T(8,128)(2,1)S(1)}, u32[]{:S(2)}, u32[]{:S(2)}) collective-permute-start(bf16[128,2,8,128]{3,2,1,0:T(8,128)(2,1)S(1)} %divide_convert_fusion), channel_id=1, source_target_pairs={{0,16},{16,32},{32,48},{48,64},{64,80},{80,96},{96,112},{112,128},... | collective-permute-start | bytes 1572872 | tf_op jit(solution)/shard_map/ppermute | solution.py:20
  230.8 16.7 %collective-permute-start.1 = (bf16[128,2,8,128]{3,2,1,0:T(8,128)(2,1)S(1)}, bf16[128,2,8,128]{3,2,1,0:T(8,128)(2,1)S(1)}, u32[]{:S(2)}, u32[]{:S(2)}) collective-permute-start(bf16[128,2,8,128]{3,2,1,0:T(8,128)(2,1)S(1)} %divide_convert_fusion), channel_id=1, source_target_pairs={{16,0},{32,16},{48,32},{64,48},{80,64},{96,80},{112,96},{128,112},... | collective-permute-start | bytes 1572872 | tf_op jit(solution)/shard_map/ppermute | solution.py:21
  249.6 14.1 %collective-permute-start.2 = (bf16[128,2,8,128]{3,2,1,0:T(8,128)(2,1)S(1)}, bf16[128,2,8,128]{3,2,1,0:T(8,128)(2,1)S(1)}, u32[]{:S(2)}, u32[]{:S(2)}) collective-permute-start(bf16[128,2,8,128]{3,2,1,0:T(8,128)(2,1)S(1)} %bitcast.33), channel_id=1, source_target_pairs={{0,1},{1,2},{2,3},{3,4},{4,5},{5,6},{6,7},{7,8},{8,9},{9,10},{10,1... | collective-permute-start | bytes 1572872 | tf_op jit(solution)/shard_map/ppermute | solution.py:20
  253.7 14.7 %collective-permute-start.3 = (bf16[128,2,8,128]{3,2,1,0:T(8,128)(2,1)S(1)}, bf16[128,2,8,128]{3,2,1,0:T(8,128)(2,1)S(1)}, u32[]{:S(2)}, u32[]{:S(2)}) collective-permute-start(bf16[128,2,8,128]{3,2,1,0:T(8,128)(2,1)S(1)} %bitcast.34), channel_id=1, source_target_pairs={{1,0},{2,1},{3,2},{4,3},{5,4},{6,5},{7,6},{8,7},{9,8},{10,9},{11,1... | collective-permute-start | bytes 1572872 | tf_op jit(solution)/shard_map/ppermute | solution.py:21
where the time goes:
time: 273 us; the launch traced here: 272 us
  waiting for transfers between devices  203 us (74%)
  local copies, waits for them, and re-layouts  27.8 us (10%)
  starting transfers between devices  25.8 us (9%)
  other arithmetic  5.77 us (2%)
  matrix products  4.88 us (2%)
  between operations  4.08 us (1%)
    all_to_all x1, waiting for transfers between devices, per_device(): lax.all_to_all(pieces, 'ev', split_axis=3, concat_axis=3, tiled=True)  182 us
    ppermute x2, waiting for transfers between devices, with_halo(): after = lax.ppermute(initial, axis, down)  15.3 us
    another operation x1, local copies, waits for them, and re-layouts, per_device(): pieces = own_part.reshape(slab_x, kernels, planes, groups, slab_y)  12.7 us
    unnamed x12, local copies, waits for them, and re-layouts  12.6 us
    ppermute x2, starting transfers between devices, with_halo(): before = lax.ppermute(last, axis, up)  11.4 us
    all_to_all x1, starting transfers between devices, per_device(): lax.all_to_all(pieces, 'ev', split_axis=3, concat_axis=3, tiled=True)  8.57 us
    ppermute x2, waiting for transfers between devices, with_halo(): before = lax.ppermute(last, axis, up)  6.16 us
    ppermute x2, starting transfers between devices, with_halo(): after = lax.ppermute(initial, axis, down)  5.79 us
  transfers between devices with their start and end apart: 5, of which 5 were waited for; matrix products, arithmetic and copies ran while one was open for 1% of the time, Pallas kernels for 0%

commit v1 on v0

v1 whole, which is shorter than its diff:
```python
import functools

import jax
import jax.numpy as jnp
from jax import lax
from jax.experimental import pallas as pl
from jax.experimental.pallas import tpu as pltpu
from jax.sharding import PartitionSpec as P

BAND = 128
blend_weight = 0.25
soft_bound = 2.0
MESH = pl.DeviceIdType.MESH
bf16, f32 = jnp.bfloat16, jnp.float32

RING = 4
LINE = 4
CHUNKS = ((0, 0, 64), (0, 64, 64), (1, 0, 64), (1, 64, 32), (1, 96, 32))
HALVES = 2
LINE_DTYPE = jnp.bfloat16
SEMS = 200


def window(first, length, fraction, along_rows, i, j):
    offset = (i + BAND - j).astype(f32)
    source = first - BAND + j
    inside = (jnp.abs(offset) <= BAND) & (source >= 0) & (source < length)
    distance = offset / (fraction * BAND)
    gaussian = jnp.where(inside, jnp.exp(-0.5 * distance * distance), 0.0)
    gaussian = gaussian / jnp.sum(gaussian, axis=along_rows, keepdims=True)
    return (gaussian + jnp.where(offset == 0.0, blend_weight, 0.0)).astype(bf16)


def kernel(
    sizes, x_hbm, ill_ref, cx_ref, cy_ref, wx_ref, wy_ref, out_ref,
    own, nxt, got, ym, yp, left, right, line, cells, xe, be, mx, my, cyt, sem,
):
    owners, groups = sizes
    slab, kernels, planes, full_y = x_hbm.shape
    block = full_y // groups
    span = block * LINE
    count = mx.shape[0] // slab
    g, e = lax.axis_index("gx"), lax.axis_index("ev")
    y, z = lax.div(e, LINE), lax.rem(e, LINE)
    up, down, across = (lax.rem(y + d, RING) for d in (1, RING - 1, 2))
    e_up, e_down = up * LINE + z, down * LINE + z

    index = {}

    def s(*key):
        return sem.at[index.setdefault(key, len(index))]

    drains = []

    def send(src, dst, name, to, cond=None):
        def make():
            return pltpu.make_async_remote_copy(
                src_ref=src(), dst_ref=dst(), send_sem=s("send", *name), recv_sem=s("recv", *name),
                device_id=to, device_id_type=MESH,
            )

        if cond is None:
            make().start()
        else:
            pl.when(cond)(lambda: make().start())
        drains.append((cond, lambda: make().wait_send()))

    def await_recv(dst, name, cond=None):
        def wait():
            pltpu.make_async_copy(dst, dst, s("recv", *name)).wait()

        if cond is None:
            wait()
        else:
            pl.when(cond)(wait)

    barrier = pltpu.get_barrier_semaphore()
    pl.semaphore_signal(barrier, inc=1, device_id={"ev": e_up}, device_id_type=MESH)
    pl.semaphore_signal(barrier, inc=1, device_id={"ev": e_down}, device_id_type=MESH)
    peers = 2
    for cond, to in (
        (e < groups - 1, {"ev": e + 1}),
        (e > 0, {"ev": e - 1}),
        (g < owners - 1, {"gx": g + 1}),
        (g > 0, {"gx": g - 1}),
    ):
        pl.when(cond)(
            functools.partial(pl.semaphore_signal, barrier, inc=1, device_id=to, device_id_type=MESH)
        )
        peers = peers + cond.astype(jnp.int32)
    pl.semaphore_wait(barrier, peers)

    def cols(target):
        return pl.ds(pl.multiple_of(target * span, span), span)

    def send_across(c):
        k, x0, n = CHUNKS[c]
        h = n // 2
        lo, hi = pl.ds(x0, h), pl.ds(x0 + h, h)
        send(lambda: x_hbm.at[lo, k, :, cols(across)], lambda: got.at[k, lo], ("a+", c), {"ev": e_up})
        send(lambda: x_hbm.at[hi, k, :, cols(across)], lambda: got.at[k, hi], ("a-", c), {"ev": e_down})

    def send_raw(c):
        k, x0, n = CHUNKS[c]
        h = n // 2
        lo, hi = pl.ds(x0, h), pl.ds(x0 + h, h)
        send(lambda: x_hbm.at[hi, k, :, cols(up)], lambda: ym.at[k, hi], ("r+", c), {"ev": e_up})
        send(lambda: x_hbm.at[lo, k, :, cols(down)], lambda: yp.at[k, lo], ("r-", c), {"ev": e_down})

    def loads(c):
        k, x0, n = CHUNKS[c]
        h = n // 2
        lo, hi, rows = pl.ds(x0, h), pl.ds(x0 + h, h), pl.ds(x0, n)
        return (
            pltpu.make_async_copy(x_hbm.at[lo, k, :, cols(up)], nxt.at[k, lo], s("nxt+", c)),
            pltpu.make_async_copy(x_hbm.at[hi, k, :, cols(down)], nxt.at[k, hi], s("nxt-", c)),
            pltpu.make_async_copy(x_hbm.at[rows, k, :, cols(y)], own.at[k, rows], s("own", c)),
        )

    def ring_stage(c):
        k, x0, n = CHUNKS[c]
        h = n // 2
        lo, hi = pl.ds(x0, h), pl.ds(x0 + h, h)
        for copy in loads(c)[:2]:
            copy.wait()
        await_recv(got.at[k, lo], ("a+", c))
        await_recv(got.at[k, hi], ("a-", c))

        def add(t, carry):
            r = pl.ds(x0 + 4 * t, 4)
            nxt[k, r] = (nxt[k, r].astype(f32) + got[k, r].astype(f32)).astype(bf16)
            return carry

        lax.fori_loop(0, n // 4, add, 0)
        send(lambda: nxt.at[k, lo], lambda: ym.at[k, lo], ("s+", c), {"ev": e_up})
        send(lambda: nxt.at[k, hi], lambda: yp.at[k, hi], ("s-", c), {"ev": e_down})

    def ring_done(c):
        k, x0, n = CHUNKS[c]
        h = n // 2
        lo, hi = pl.ds(x0, h), pl.ds(x0 + h, h)
        loads(c)[2].wait()
        await_recv(ym.at[k, hi], ("r+", c))
        await_recv(yp.at[k, lo], ("r-", c))
        await_recv(ym.at[k, lo], ("s+", c))
        await_recv(yp.at[k, hi], ("s-", c))

    def unit(c, target, rightward, first, slot):
        k, x0, n = CHUNKS[c]
        lanes = pl.ds(target * block, block)
        arrived = left if rightward else right
        name = ("l" if rightward else "r", c, target)
        rows = pl.ds(x0, n)
        if not first:
            await_recv(arrived.at[k, rows, :, lanes], name)

        def add(t, carry):
            r = pl.ds(x0 + 8 * t, 8)
            total = own[k, r, :, lanes].astype(f32) + ym[k, r, :, lanes].astype(f32)
            total = total + yp[k, r, :, lanes].astype(f32)
            if not first:
                total = total + arrived[k, r, :, lanes].astype(f32)
            line[k, r, :, lanes] = total.astype(line.dtype)
            return carry

        lax.fori_loop(0, n // 8, add, 0)
        make = lambda: pltpu.make_async_remote_copy(
            src_ref=line.at[k, rows, :, lanes], dst_ref=arrived.at[k, rows, :, lanes],
            send_sem=s("linesend", c, slot), recv_sem=s("recv", *name),
            device_id={"ev": e + 1 if rightward else e - 1}, device_id_type=MESH,
        )
        make().start()
        return lambda: make().wait_send()

    line_drains = {at: [] for at in range(LINE)}

    def line_stage(c, plan):
        for at, units in plan.items():
            def run(at=at, units=units):
                for target, rightward, first, slot in units:
                    line_drains[at].append(unit(c, target, rightward, first, slot))
            pl.when(z == at)(run)

    hop0 = {0: [(t, True, True, 3 - t) for t in (3, 2, 1)], 3: [(t, False, True, t) for t in (0, 1, 2)]}
    hop1 = {1: [(3, True, False, 0), (2, True, False, 1)], 2: [(0, False, False, 0), (1, False, False, 1)]}
    hop2 = {2: [(3, True, False, 2)], 1: [(0, False, False, 2)]}

    def finish(c):
        k, x0, n = CHUNKS[c]
        rows = pl.ds(x0, n)
        lanes = pl.ds(pl.multiple_of(z * block, block), block)
        for at in range(LINE):
            here = pl.ds(at * block, block)
            if at > 0:
                await_recv(left.at[k, rows, :, here], ("l", c, at), z == at)
            if at < LINE - 1:
                await_recv(right.at[k, rows, :, here], ("r", c, at), z == at)

        def add(t, carry):
            r = pl.ds(x0 + 8 * t, 8)
            total = own[k, r, :, lanes].astype(f32) + ym[k, r, :, lanes].astype(f32)
            total = total + yp[k, r, :, lanes].astype(f32)
            total = total + left[k, r, :, lanes].astype(f32) + right[k, r, :, lanes].astype(f32)
            cells[pl.ds(64 * t, 64), :] = (total / ill_ref[r]).reshape(8 * planes, block)
            return carry

        lax.fori_loop(0, n // 8, add, 0)
        for plane in range(planes):
            xe[k, plane, pl.ds(slab + x0, n), :] = cells[pl.ds(plane, n, stride=planes), :].astype(bf16)
        src = lambda: xe.at[k, :, pl.ds(slab + x0, n), :]
        send(src, lambda: xe.at[k, :, pl.ds(x0, n), :], ("x+", c), {"gx": g + 1}, g < owners - 1)
        send(src, lambda: xe.at[k, :, pl.ds(2 * slab + x0, n), :], ("x-", c), {"gx": g - 1}, g > 0)

    def smooth_x(k):
        for c, (kc, x0, n) in enumerate(CHUNKS):
            if kc == k:
                await_recv(xe.at[k, :, pl.ds(x0, n), :], ("x+", c), g > 0)
                await_recv(xe.at[k, :, pl.ds(2 * slab + x0, n), :], ("x-", c), g < owners - 1)
        step = planes // HALVES
        for half in range(HALVES):
            def pair(t, carry, half=half):
                p = half * step + 2 * t
                data = jnp.concatenate([xe[k, p], xe[k, p + 1]], axis=1)
                labels = jnp.concatenate([cx_ref[pl.ds(p, 1), :], cx_ref[pl.ds(p + 1, 1), :]], axis=1)
                product = jnp.dot(mx[...], data, preferred_element_type=f32)
                total = product[:slab]
                for level in range(1, count):
                    total = jnp.where(labels == level, product[level * slab : (level + 1) * slab], total)
                bounded = (soft_bound * jnp.tanh(total / soft_bound)).astype(bf16)
                be[k, 1, p] = bounded[:, :block]
                be[k, 1, p + 1] = bounded[:, block:]
                return carry

            lax.fori_loop(0, step // 2, pair, 0)
            part = pl.ds(half * step, step)
            src = lambda part=part: be.at[k, 1, part]
            send(src, lambda part=part: be.at[k, 0, part], ("y+", k, half), {"ev": e + 1}, e < groups - 1)
            send(src, lambda part=part: be.at[k, 2, part], ("y-", k, half), {"ev": e - 1}, e > 0)

    def smooth_y(k):
        step = planes // HALVES
        for half in range(HALVES):
            part = pl.ds(half * step, step)
            await_recv(be.at[k, 0, part], ("y+", k, half), e > 0)
            await_recv(be.at[k, 2, part], ("y-", k, half), e < groups - 1)

            def pair(t, carry, half=half):
                p = half * step + 2 * t
                two = pl.ds(p, 2)
                data = jnp.concatenate([be[k, side, two].reshape(2 * slab, block) for side in range(3)], axis=1)
                product = jnp.dot(data, my[...], preferred_element_type=f32)
                labels = cyt[two].reshape(2 * slab, block)
                total = product[:, :block]
                for level in range(1, count):
                    total = jnp.where(labels == level, product[:, level * block : (level + 1) * block], total)
                out_ref[k, two] = total.astype(out_ref.dtype).reshape(2, slab, block)
                return carry

            lax.fori_loop(0, step // 2, pair, 0)

    def prepare():
        i = lax.broadcasted_iota(jnp.int32, (slab, slab + 2 * BAND), 0)
        j = lax.broadcasted_iota(jnp.int32, (slab, slab + 2 * BAND), 1)
        for level in range(count):
            mx[level * slab : (level + 1) * slab, :] = window(g * slab, slab * owners, wx_ref[level], 1, i, j)
        j = lax.broadcasted_iota(jnp.int32, (block + 2 * BAND, block), 0)
        i = lax.broadcasted_iota(jnp.int32, (block + 2 * BAND, block), 1)
        for level in range(count):
            my[:, level * block : (level + 1) * block] = window(e * block, full_y, wy_ref[level], 0, i, j)
        for plane in range(planes):
            row = cy_ref[plane : plane + 1, :].astype(f32)
            cyt[plane] = jnp.broadcast_to(row, (slab, slab)).T

        def zero(ref):
            def fill():
                ref[...] = jnp.zeros(ref.shape, ref.dtype)
            return fill

        pl.when(z == 0)(zero(left.at[:, :, :, pl.ds(0, block)]))
        pl.when(z == LINE - 1)(zero(right.at[:, :, :, pl.ds((LINE - 1) * block, block)]))
        pl.when(g == 0)(zero(xe.at[:, :, pl.ds(0, slab), :]))
        pl.when(g == owners - 1)(zero(xe.at[:, :, pl.ds(2 * slab, slab), :]))
        pl.when(e == 0)(zero(be.at[:, 0]))
        pl.when(e == groups - 1)(zero(be.at[:, 2]))

    total_chunks = len(CHUNKS)
    send_across(0)
    send_raw(0)
    send_across(1)
    for c in range(total_chunks):
        for copy in loads(c):
            copy.start()
    prepare()
    ready = {}
    for k in range(kernels):
        ready[k] = max(c for c in range(total_chunks) if CHUNKS[c][0] == k) + 3
    for slot in range(total_chunks + 4):
        if slot < total_chunks:
            ring_stage(slot)
            if slot + 1 < total_chunks:
                send_raw(slot + 1)
            if slot + 2 < total_chunks:
                send_across(slot + 2)
        if 0 <= slot - 1 < total_chunks:
            ring_done(slot - 1)
            line_stage(slot - 1, hop0)
        if 0 <= slot - 2 < total_chunks:
            line_stage(slot - 2, hop2)
            finish(slot - 2)
        if 0 <= slot - 1 < total_chunks:
            line_stage(slot - 1, hop1)
        for k in range(kernels):
            if slot == ready[k]:
                smooth_x(k)
            if slot == ready[k] + 1:
                smooth_y(k)

    for cond, drain in drains:
        if cond is None:
            drain()
        else:
            pl.when(cond)(drain)
    for at, waits in line_drains.items():
        def run(waits=waits):
            for wait in waits:
                wait()
        pl.when(z == at)(run)
    assert len(index) <= SEMS


def per_device(partial_kernels, illumination, classes_x, classes_y, widths_x, widths_y):
    own_part = partial_kernels[0]
    slab, kernels, planes, full_y = own_part.shape
    groups, owners = lax.axis_size("ev"), lax.axis_size("gx")
    block = full_y // groups
    span = block * LINE
    count = widths_x.shape[0]
    vmem, smem = pl.BlockSpec(memory_space=pltpu.VMEM), pl.BlockSpec(memory_space=pltpu.SMEM)
    wide = (kernels, slab, planes, span)
    out = pl.pallas_call(
        functools.partial(kernel, (owners, groups)),
        out_shape=jax.ShapeDtypeStruct((kernels, planes, slab, block), bf16),
        in_specs=[pl.BlockSpec(memory_space=pl.ANY), vmem, vmem, vmem, smem, smem],
        out_specs=vmem,
        scratch_shapes=[
            pltpu.VMEM(wide, bf16),
            pltpu.VMEM(wide, bf16),
            pltpu.VMEM(wide, bf16),
            pltpu.VMEM(wide, bf16),
            pltpu.VMEM(wide, bf16),
            pltpu.VMEM(wide, LINE_DTYPE),
            pltpu.VMEM(wide, LINE_DTYPE),
            pltpu.VMEM(wide, LINE_DTYPE),
            pltpu.VMEM((64 * planes, block), f32),
            pltpu.VMEM((kernels, planes, 3 * slab, block), bf16),
            pltpu.VMEM((kernels, 3, planes, slab, block), bf16),
            pltpu.VMEM((count * slab, slab + 2 * BAND), bf16),
            pltpu.VMEM((block + 2 * BAND, count * block), bf16),
            pltpu.VMEM((planes, slab, slab), f32),
            pltpu.SemaphoreType.DMA((SEMS,)),
        ],
        compiler_params=pltpu.CompilerParams(
            collective_id=0, has_side_effects=True, vmem_limit_bytes=56 * 1024 * 1024
        ),
        cost_estimate=pl.CostEstimate(flops=2_000_000_000, bytes_accessed=16_000_000, transcendentals=300_000),
        name="condition",
    )(own_part, illumination, classes_x, classes_y.T, widths_x, widths_y)
    return out.transpose(2, 0, 1, 3)


def solution(mesh):
    return jax.shard_map(
        per_device,
        mesh=mesh,
        in_specs=(
            P("ev", "gx", None, None, None),
            P("gx", None, "ev"),
            P(None, "ev"),
            P("gx", None),
            P(),
            P(),
        ),
        out_specs=P("gx", None, None, "ev"),
        check_vma=False,
    )
```

time: 273 us -> 120 us (0.44)
  waiting for transfers between devices: 203 us -> 0 us
  Pallas kernels: 0 us -> 116 us
  starting transfers between devices: 25.8 us -> 0 us
  local copies, waits for them, and re-layouts: 27.8 us -> 2.18 us
  other arithmetic: 5.77 us -> 0 us
  matrix products: 4.88 us -> 0 us
  between operations: 4.08 us -> 0.01 us
    all_to_all x1 -> x0, waiting for transfers between devices: 182 us -> none  [per_device(): lax.all_to_all(pieces, 'ev', split_axis=3, concat_axis=3, tiled=True)]
    pallas_call x0 -> x1, Pallas kernels: none -> 116 us  [per_device(): pl.pallas_call(functools.partial(kernel, (owners, groups)), out_shape=jax...]
    ppermute x4 -> x0, waiting for transfers between devices: 21.5 us -> none  [the longest x2 15.3 us: with_halo(): after = lax.ppermute(initial, axis, down)]
    ppermute x4 -> x0, starting transfers between devices: 17.2 us -> none  [the longest x2 11.4 us: with_halo(): before = lax.ppermute(last, axis, up)]
    another operation x1 -> x0, local copies, waits for them, and re-layouts: 12.7 us -> none  [per_device(): pieces = own_part.reshape(slab_x, kernels, planes, groups, slab_y)]
    unnamed x12 -> x0, local copies, waits for them, and re-layouts: 12.6 us -> none
    all_to_all x1 -> x0, starting transfers between devices: 8.57 us -> none  [per_device(): lax.all_to_all(pieces, 'ev', split_axis=3, concat_axis=3, tiled=True)]
    reduce_sum x3 -> x0, other arithmetic: 5.37 us -> none  [the longest x1 4.67 us: per_device(): summed = jnp.sum(arrived.astype(jnp.float32), axis=3)]
  transfers between devices with their start and end apart: 5 -> 0, of which waited for: 5 -> 0; matrix products, arithmetic and copies ran while one was open for 1% -> 0% of each run, Pallas kernels for 0% -> 0%
where the time goes in v1:
time: 120 us; the launch traced here: 118 us
  Pallas kernels  116 us (97%)
  local copies, waits for them, and re-layouts  2.18 us (2%)
    pallas_call x1, Pallas kernels, per_device(): pl.pallas_call(functools.partial(kernel, (owners, groups)), out_shape=jax...  116 us

profile of v1, /device:TPU:15, one launch (start us, length us, event | category | flops | bytes accessed | tf_op | source)
XLA Modules:
  0.0 118.4 jit_solution(16903087966874443016)
XLA Ops:
  0.0 116.2 %condition.1 = bf16[2,8,128,128]{3,2,1,0:T(8,128)(2,1)} custom-call(bf16[128,2,8,2048]{3,2,1,0:T(8,128)(2,1)} %bitcast.3, f32[128,8,128]{2,1,0:T(8,128)} %ill_ref.1, s32[8,128]{1,0:T(8,128)} %cx_ref.1, s32[8,128]{1,0:T(8,128)} %bitcast.5, f32[3]{0:T(128)} %wx_ref.1, f32[3]{0:T(128)} %wy_ref.1), custom_call_target="tpu_custom_call" | custom-call | flops 2000000000 | bytes 16000000 | tf_op jit(solution)/shard_map/condition/pallas_call | solution.py:340
  116.2 2.2 %copy.7 = bf16[128,2,8,128]{3,2,1,0:T(8,128)(2,1)} copy(bf16[128,2,8,128]{3,0,2,1:T(8,128)(2,1)} %bitcast.4) | data formatting | bytes 1048576 | tf_op jit(solution)/shard_map/transpose | solution.py:368

commit v2 on v1

v2 whole, which is shorter than its diff:
```python
import functools

import jax
import jax.numpy as jnp
from jax import lax
from jax.experimental import pallas as pl
from jax.experimental.pallas import tpu as pltpu
from jax.sharding import PartitionSpec as P

BAND = 128
blend_weight = 0.25
soft_bound = 2.0
MESH = pl.DeviceIdType.MESH
bf16, f32 = jnp.bfloat16, jnp.float32

RING = 4
LINE = 4
PLANES = 4
CHUNKS = ((0, 0, 32), (0, 32, 32), (1, 0, 32), (1, 32, 32), (2, 0, 32), (2, 32, 32), (3, 0, 32), (3, 32, 16), (3, 48, 16))
SEMS = 320


def window(first, length, fraction, along_rows, i, j):
    offset = (i + BAND - j).astype(f32)
    source = first - BAND + j
    inside = (jnp.abs(offset) <= BAND) & (source >= 0) & (source < length)
    distance = offset / (fraction * BAND)
    gaussian = jnp.where(inside, jnp.exp(-0.5 * distance * distance), 0.0)
    gaussian = gaussian / jnp.sum(gaussian, axis=along_rows, keepdims=True)
    return (gaussian + jnp.where(offset == 0.0, blend_weight, 0.0)).astype(bf16)


def kernel(
    sizes, x_hbm, ill_hbm, cx_ref, cy_ref, wx_ref, wy_ref, out_ref,
    own, nxt, got, ym, yp, left16, right16, line16, left32, right32, line32, ill, cells, xe, be, mx, my, cyt, sem,
):
    owners, groups = sizes
    slab, kernels, planes, full_y = x_hbm.shape
    block = full_y // groups
    span = block * LINE
    half = slab // 2
    count = mx.shape[0] // slab
    per_kernel = planes // PLANES
    pieces = kernels * per_kernel
    g, e = lax.axis_index("gx"), lax.axis_index("ev")
    y, z = lax.div(e, LINE), lax.rem(e, LINE)
    up, down, across = (lax.rem(y + d, RING) for d in (1, RING - 1, 2))
    e_up, e_down = up * LINE + z, down * LINE + z

    index = {}

    def s(*key):
        return sem.at[index.setdefault(key, len(index))]

    drains = []

    def when(cond, action):
        if cond is None:
            action()
        else:
            pl.when(cond)(action)

    def send(src, dst, name, to, cond=None):
        def make():
            return pltpu.make_async_remote_copy(
                src_ref=src(), dst_ref=dst(), send_sem=s("send", *name), recv_sem=s("recv", *name),
                device_id=to, device_id_type=MESH,
            )

        when(cond, lambda: make().start())
        drains.append((cond, lambda: make().wait_send()))

    def await_recv(dst, name, cond=None):
        when(cond, lambda: pltpu.make_async_copy(dst, dst, s("recv", *name)).wait())

    barrier = pltpu.get_barrier_semaphore()
    pl.semaphore_signal(barrier, inc=1, device_id={"ev": e_up}, device_id_type=MESH)
    pl.semaphore_signal(barrier, inc=1, device_id={"ev": e_down}, device_id_type=MESH)
    peers = 2
    for cond, to in (
        (e < groups - 1, {"ev": e + 1}),
        (e > 0, {"ev": e - 1}),
        (g < owners - 1, {"gx": g + 1}),
        (g > 0, {"gx": g - 1}),
    ):
        pl.when(cond)(
            functools.partial(pl.semaphore_signal, barrier, inc=1, device_id=to, device_id_type=MESH)
        )
        peers = peers + cond.astype(jnp.int32)
    pl.semaphore_wait(barrier, peers)

    def term(chunk, side, target):
        p, r0, n = chunk
        lanes = pl.ds(pl.multiple_of(target * span, span), span)
        first = (p % per_kernel) * PLANES
        return x_hbm.at[pl.ds(side * half + r0, n), p // per_kernel, pl.ds(first, PLANES), lanes]

    def part(ref, chunk, side):
        p, r0, n = chunk
        return ref.at[p, pl.ds(r0, n), pl.ds(side * PLANES, PLANES), :]

    def send_across(c):
        chunk = CHUNKS[c]
        send(lambda: term(chunk, 0, across), lambda: part(got, chunk, 0), ("a+", c), {"ev": e_up})
        send(lambda: term(chunk, 1, across), lambda: part(got, chunk, 1), ("a-", c), {"ev": e_down})

    def send_raw(c):
        chunk = CHUNKS[c]
        send(lambda: term(chunk, 1, up), lambda: part(ym, chunk, 1), ("r+", c), {"ev": e_up})
        send(lambda: term(chunk, 0, down), lambda: part(yp, chunk, 0), ("r-", c), {"ev": e_down})

    def loads(c):
        chunk = CHUNKS[c]
        for side, ref, target, name in (
            (0, nxt, up, "n0"), (1, nxt, down, "n1"), (0, own, y, "o0"), (1, own, y, "o1"),
        ):
            yield name, lambda side=side, ref=ref, target=target, name=name: pltpu.make_async_copy(
                term(chunk, side, target), part(ref, chunk, side), s(name, c)
            )

    def ring_stage(c):
        chunk = p, r0, n = CHUNKS[c]
        for name, make in loads(c):
            if name[0] == "n":
                make().wait()
        await_recv(part(got, chunk, 0), ("a+", c))
        await_recv(part(got, chunk, 1), ("a-", c))

        def add(t, carry):
            r = pl.ds(r0 + 4 * t, 4)
            nxt[p, r] = (nxt[p, r].astype(f32) + got[p, r].astype(f32)).astype(bf16)
            return carry

        lax.fori_loop(0, n // 4, add, 0)
        send(lambda: part(nxt, chunk, 0), lambda: part(ym, chunk, 0), ("s+", c), {"ev": e_up})
        send(lambda: part(nxt, chunk, 1), lambda: part(yp, chunk, 1), ("s-", c), {"ev": e_down})

    def ring_done(c):
        chunk = CHUNKS[c]
        for name, make in loads(c):
            if name[0] == "o":
                make().wait()
        await_recv(part(ym, chunk, 1), ("r+", c))
        await_recv(part(yp, chunk, 0), ("r-", c))
        await_recv(part(ym, chunk, 0), ("s+", c))
        await_recv(part(yp, chunk, 1), ("s-", c))

    def unit(c, at, target, slot):
        p, r0, n = CHUNKS[c]
        rightward = target > at
        first = at == (0 if rightward else LINE - 1)
        lanes = pl.ds(target * block, block)
        rows = pl.ds(r0, n)
        name = ("l" if rightward else "r", c, target)

        def landing(source):
            short = source in (0, LINE - 1) and abs(target - source) > 1
            if rightward:
                return left16 if short else left32
            return right16 if short else right32

        arrived = landing(at - 1 if rightward else at + 1)
        to = landing(at)
        staged = line16 if to.dtype == bf16 else line32
        if not first:
            await_recv(arrived.at[p, rows, :, lanes], name)

        def add(t, carry):
            r = pl.ds(r0 + 8 * t, 8)
            total = own[p, r, :, lanes].astype(f32) + ym[p, r, :, lanes].astype(f32)
            total = total + yp[p, r, :, lanes].astype(f32)
            if not first:
                total = total + arrived[p, r, :, lanes].astype(f32)
            staged[p, r, :, lanes] = total.astype(staged.dtype)
            return carry

        lax.fori_loop(0, n // 8, add, 0)
        make = lambda: pltpu.make_async_remote_copy(
            src_ref=staged.at[p, rows, :, lanes], dst_ref=to.at[p, rows, :, lanes],
            send_sem=s("linesend", c, slot), recv_sem=s("recv", *name),
            device_id={"ev": e + 1 if rightward else e - 1}, device_id_type=MESH,
        )
        make().start()
        return lambda: make().wait_send()

    line_drains = {at: [] for at in range(LINE)}

    def line_stage(c, plan):
        for at, units in plan.items():
            def run(at=at, units=units):
                for target, slot in units:
                    line_drains[at].append(unit(c, at, target, slot))
            pl.when(z == at)(run)

    hop0 = {0: [(3, 0), (2, 1), (1, 2)], 3: [(0, 0), (1, 1), (2, 2)]}
    hop1 = {1: [(3, 0), (2, 1)], 2: [(0, 0), (1, 1)]}
    hop2 = {2: [(3, 2)], 1: [(0, 2)]}

    def finish(c):
        p, r0, n = CHUNKS[c]
        zg = p % per_kernel
        rows = pl.ds(r0, n)
        lanes = pl.ds(pl.multiple_of(z * block, block), block)
        for at in range(LINE):
            here = pl.ds(at * block, block)
            if at > 0:
                await_recv(left32.at[p, rows, :, here], ("l", c, at), z == at)
            if at < LINE - 1:
                await_recv(right32.at[p, rows, :, here], ("r", c, at), z == at)

        def add(t, carry):
            r = pl.ds(r0 + 8 * t, 8)
            total = own[p, r, :, lanes].astype(f32) + ym[p, r, :, lanes].astype(f32)
            total = total + yp[p, r, :, lanes].astype(f32)
            total = total + left32[p, r, :, lanes] + right32[p, r, :, lanes]
            cells[pl.ds(16 * PLANES * t, 16 * PLANES), :] = (total / ill[zg, r]).reshape(16 * PLANES, block)
            return carry

        lax.fori_loop(0, n // 8, add, 0)
        for side in range(2):
            for plane in range(PLANES):
                picked = cells[pl.ds(side * PLANES + plane, n, stride=2 * PLANES), :]
                xe[p, plane, 2 + side, rows, :] = picked.astype(bf16)
        src = lambda: xe.at[p, :, pl.ds(2, 2), rows, :]
        send(src, lambda: xe.at[p, :, pl.ds(0, 2), rows, :], ("x+", c), {"gx": g + 1}, g < owners - 1)
        send(src, lambda: xe.at[p, :, pl.ds(4, 2), rows, :], ("x-", c), {"gx": g - 1}, g > 0)

    def smooth_x(p):
        zg = p % per_kernel
        for c, (pc, r0, n) in enumerate(CHUNKS):
            if pc == p:
                await_recv(xe.at[p, :, pl.ds(0, 2), pl.ds(r0, n), :], ("x+", c), g > 0)
                await_recv(xe.at[p, :, pl.ds(4, 2), pl.ds(r0, n), :], ("x-", c), g < owners - 1)
        for a in range(0, PLANES, 2):
            data = jnp.concatenate([xe[p, b].reshape(3 * slab, block) for b in (a, a + 1)], axis=1)
            d = zg * PLANES + a
            labels = jnp.concatenate([cx_ref[d : d + 1, :], cx_ref[d + 1 : d + 2, :]], axis=1)
            product = jnp.dot(mx[...], data, preferred_element_type=f32)
            total = product[:slab]
            for level in range(1, count):
                total = jnp.where(labels == level, product[level * slab : (level + 1) * slab], total)
            bounded = (soft_bound * jnp.tanh(total / soft_bound)).astype(bf16)
            be[p, 1, a] = bounded[:, :block]
            be[p, 1, a + 1] = bounded[:, block:]
            two = pl.ds(a, 2)
            src = lambda two=two: be.at[p, 1, two]
            send(src, lambda two=two: be.at[p, 0, two], ("y+", p, a), {"ev": e + 1}, e < groups - 1)
            send(src, lambda two=two: be.at[p, 2, two], ("y-", p, a), {"ev": e - 1}, e > 0)

    def smooth_y(p):
        k, zg = p // per_kernel, p % per_kernel
        for a in range(0, PLANES, 2):
            two = pl.ds(a, 2)
            await_recv(be.at[p, 0, two], ("y+", p, a), e > 0)
            await_recv(be.at[p, 2, two], ("y-", p, a), e < groups - 1)
            data = jnp.concatenate([be[p, side, two].reshape(2 * slab, block) for side in range(3)], axis=1)
            product = jnp.dot(data, my[...], preferred_element_type=f32)
            deep = pl.ds(zg * PLANES + a, 2)
            labels = cyt[deep].reshape(2 * slab, block)
            total = product[:, :block]
            for level in range(1, count):
                total = jnp.where(labels == level, product[:, level * block : (level + 1) * block], total)
            out_ref[k, deep] = total.astype(out_ref.dtype).reshape(2, slab, block)

    def prepare():
        i = lax.broadcasted_iota(jnp.int32, (slab, slab + 2 * BAND), 0)
        j = lax.broadcasted_iota(jnp.int32, (slab, slab + 2 * BAND), 1)
        for level in range(count):
            mx[level * slab : (level + 1) * slab, :] = window(g * slab, slab * owners, wx_ref[level], 1, i, j)
        j = lax.broadcasted_iota(jnp.int32, (block + 2 * BAND, block), 0)
        i = lax.broadcasted_iota(jnp.int32, (block + 2 * BAND, block), 1)
        for level in range(count):
            my[:, level * block : (level + 1) * block] = window(e * block, full_y, wy_ref[level], 0, i, j)
        for plane in range(planes):
            row = cy_ref[plane : plane + 1, :].astype(f32)
            cyt[plane] = jnp.broadcast_to(row, (slab, slab)).T

        def zero(ref):
            def fill():
                ref[...] = jnp.zeros(ref.shape, ref.dtype)
            return fill

        pl.when(z == 0)(zero(left32.at[:, :, :, pl.ds(0, block)]))
        pl.when(z == LINE - 1)(zero(right32.at[:, :, :, pl.ds((LINE - 1) * block, block)]))
        pl.when(g == 0)(zero(xe.at[:, :, pl.ds(0, 2)]))
        pl.when(g == owners - 1)(zero(xe.at[:, :, pl.ds(4, 2)]))
        pl.when(e == 0)(zero(be.at[:, 0]))
        pl.when(e == groups - 1)(zero(be.at[:, 2]))

    def ill_loads():
        for zg in range(per_kernel):
            for side in range(2):
                yield lambda zg=zg, side=side: pltpu.make_async_copy(
                    ill_hbm.at[pl.ds(side * half, half), pl.ds(zg * PLANES, PLANES), :],
                    ill.at[zg, :, pl.ds(side * PLANES, PLANES), :], s("ill", zg, side),
                )

    chunks = len(CHUNKS)
    send_across(0)
    send_raw(0)
    send_across(1)
    for c in range(chunks):
        for name, make in loads(c):
            make().start()
    for make in ill_loads():
        make().start()
    ready = [max(c for c in range(chunks) if CHUNKS[c][0] == p) + 3 for p in range(pieces)]
    for slot in range(chunks + 4):
        if slot < chunks:
            ring_stage(slot)
            if slot + 1 < chunks:
                send_raw(slot + 1)
            if slot + 2 < chunks:
                send_across(slot + 2)
        if slot == 0:
            prepare()
            for make in ill_loads():
                make().wait()
        if 0 <= slot - 1 < chunks:
            ring_done(slot - 1)
            line_stage(slot - 1, hop0)
        if 0 <= slot - 2 < chunks:
            line_stage(slot - 2, hop2)
        if 0 <= slot - 1 < chunks:
            line_stage(slot - 1, hop1)
        if 0 <= slot - 2 < chunks:
            finish(slot - 2)
        for p in range(pieces):
            if slot == ready[p]:
                smooth_x(p)
        for p in range(pieces):
            if slot == (ready[-1] if p == pieces - 2 else ready[p] + (1 if p == pieces - 1 else 2)):
                smooth_y(p)

    for cond, drain in drains:
        when(cond, drain)
    for at, waits in line_drains.items():
        def run(waits=waits):
            for wait in waits:
                wait()
        pl.when(z == at)(run)
    assert len(index) <= SEMS, len(index)


def per_device(partial_kernels, illumination, classes_x, classes_y, widths_x, widths_y):
    own_part = partial_kernels[0]
    slab, kernels, planes, full_y = own_part.shape
    groups, owners = lax.axis_size("ev"), lax.axis_size("gx")
    block = full_y // groups
    span = block * LINE
    count = widths_x.shape[0]
    pieces = kernels * planes // PLANES
    vmem, smem = pl.BlockSpec(memory_space=pltpu.VMEM), pl.BlockSpec(memory_space=pltpu.SMEM)
    hbm = pl.BlockSpec(memory_space=pl.ANY)
    wide = (pieces, slab // 2, 2 * PLANES, span)
    out = pl.pallas_call(
        functools.partial(kernel, (owners, groups)),
        out_shape=jax.ShapeDtypeStruct((kernels, planes, slab, block), bf16),
        in_specs=[hbm, hbm, vmem, vmem, smem, smem],
        out_specs=vmem,
        scratch_shapes=[pltpu.VMEM(wide, bf16)] * 8
        + [pltpu.VMEM(wide, f32)] * 3
        + [
            pltpu.VMEM((planes // PLANES, slab // 2, 2 * PLANES, block), f32),
            pltpu.VMEM((slab * PLANES, block), f32),
            pltpu.VMEM((pieces, PLANES, 6, slab // 2, block), bf16),
            pltpu.VMEM((pieces, 3, PLANES, slab, block), bf16),
            pltpu.VMEM((count * slab, slab + 2 * BAND), bf16),
            pltpu.VMEM((block + 2 * BAND, count * block), bf16),
            pltpu.VMEM((planes, slab, slab), f32),
            pltpu.SemaphoreType.DMA((SEMS,)),
        ],
        compiler_params=pltpu.CompilerParams(
            collective_id=0, has_side_effects=True, vmem_limit_bytes=56 * 1024 * 1024
        ),
        cost_estimate=pl.CostEstimate(flops=2_000_000_000, bytes_accessed=16_000_000, transcendentals=300_000),
        name="condition",
    )(own_part, illumination, classes_x, classes_y.T, widths_x, widths_y)
    return out.transpose(2, 0, 1, 3)


def solution(mesh):
    return jax.shard_map(
        per_device,
        mesh=mesh,
        in_specs=(
            P("ev", "gx", None, None, None),
            P("gx", None, "ev"),
            P(None, "ev"),
            P("gx", None),
            P(),
            P(),
        ),
        out_specs=P("gx", None, None, "ev"),
        check_vma=False,
    )
```

time: 120 us -> 124 us (1.033); the launches traced: 118 us -> 124 us
  Pallas kernels: 116 us -> 122 us
    pallas_call x1, Pallas kernels: 116 us -> 122 us  [per_device(): pl.pallas_call(functools.partial(kernel, (owners, groups)), out_shape=jax...]
where the time goes in v2:
time: 124 us
  Pallas kernels  122 us (98%)
  local copies, waits for them, and re-layouts  2.18 us (2%)
    pallas_call x1, Pallas kernels, per_device(): pl.pallas_call(functools.partial(kernel, (owners, groups)), out_shape=jax...  122 us

profile of v2, /device:TPU:15, one launch (start us, length us, event | category | flops | bytes accessed | tf_op | source)
XLA Modules:
  0.0 123.8 jit_solution(18330305865389600430)
XLA Ops:
  0.0 121.6 %condition.1 = bf16[2,8,128,128]{3,2,1,0:T(8,128)(2,1)} custom-call(bf16[128,2,8,2048]{3,2,1,0:T(8,128)(2,1)} %bitcast.3, f32[128,8,128]{2,1,0:T(8,128)} %ill_hbm.1, s32[8,128]{1,0:T(8,128)} %cx_ref.1, s32[8,128]{1,0:T(8,128)} %bitcast.5, f32[3]{0:T(128)} %wx_ref.1, f32[3]{0:T(128)} %wy_ref.1), custom_call_target="tpu_custom_call" | custom-call | flops 2000000000 | bytes 16000000 | tf_op jit(solution)/shard_map/condition/pallas_call | solution.py:356
  121.7 2.2 %copy.7 = bf16[128,2,8,128]{3,2,1,0:T(8,128)(2,1)} copy(bf16[128,2,8,128]{3,0,2,1:T(8,128)(2,1)} %bitcast.4) | data formatting | bytes 1048576 | tf_op jit(solution)/shard_map/transpose | solution.py:379

commit v3 on v2

--- a/solution.py
+++ b/solution.py
@@ -16,8 +16,8 @@
 RING = 4
 LINE = 4
 PLANES = 4
-CHUNKS = ((0, 0, 32), (0, 32, 32), (1, 0, 32), (1, 32, 32), (2, 0, 32), (2, 32, 32), (3, 0, 32), (3, 32, 16), (3, 48, 16))
-SEMS = 320
+CHUNKS = ((0,0,16),(0,16,48),(1,0,32),(1,32,32),(2,0,32),(2,32,32),(3,0,32),(3,32,32))
+SEMS = 420
 
 
 def window(first, length, fraction, along_rows, i, j):
@@ -32,13 +32,15 @@
 
 def kernel(
     sizes, x_hbm, ill_hbm, cx_ref, cy_ref, wx_ref, wy_ref, out_ref,
-    own, nxt, got, ym, yp, left16, right16, line16, left32, right32, line32, ill, cells, xe, be, mx, my, cyt, sem,
+    own, nxt, got, ym, yp, via, via_out, near, near_out, far, far_out, ill, cells, xe, passed, be, mx, my, cyt, sem,
 ):
     owners, groups = sizes
     slab, kernels, planes, full_y = x_hbm.shape
     block = full_y // groups
     span = block * LINE
     half = slab // 2
+    seam_hi = owners // 2
+    seam_lo = seam_hi - 1
     count = mx.shape[0] // slab
     per_kernel = planes // PLANES
     pieces = kernels * per_kernel
@@ -46,6 +48,14 @@
     y, z = lax.div(e, LINE), lax.rem(e, LINE)
     up, down, across = (lax.rem(y + d, RING) for d in (1, RING - 1, 2))
     e_up, e_down = up * LINE + z, down * LINE + z
+    mate = z + 1 - 2 * lax.rem(z, 2)
+    at_end = (z == 0) | (z == LINE - 1)
+    inner = jnp.logical_not(at_end)
+
+    def by_way(p):
+        return 2 * p + 1, seam_hi + 2 * (p + 1)
+
+    beyond = (lax.rem(z + 2, LINE), lax.rem(mate + 2, LINE))
 
     index = {}
 
@@ -60,15 +70,15 @@
         else:
             pl.when(cond)(action)
 
-    def send(src, dst, name, to, cond=None):
-        def make():
-            return pltpu.make_async_remote_copy(
-                src_ref=src(), dst_ref=dst(), send_sem=s("send", *name), recv_sem=s("recv", *name),
-                device_id=to, device_id_type=MESH,
-            )
-
-        when(cond, lambda: make().start())
-        drains.append((cond, lambda: make().wait_send()))
+    def make_copy(src, dst, name, to, out=None):
+        return pltpu.make_async_remote_copy(
+            src_ref=src(), dst_ref=dst(), send_sem=s("send", *(out or name)), recv_sem=s("recv", *name),
+            device_id=to, device_id_type=MESH,
+        )
+
+    def send(*copy, cond=None):
+        when(cond, lambda: make_copy(*copy).start())
+        drains.append((cond, lambda: make_copy(*copy).wait_send()))
 
     def await_recv(dst, name, cond=None):
         when(cond, lambda: pltpu.make_async_copy(dst, dst, s("recv", *name)).wait())
@@ -76,7 +86,8 @@
     barrier = pltpu.get_barrier_semaphore()
     pl.semaphore_signal(barrier, inc=1, device_id={"ev": e_up}, device_id_type=MESH)
     pl.semaphore_signal(barrier, inc=1, device_id={"ev": e_down}, device_id_type=MESH)
-    peers = 2
+    pl.semaphore_signal(barrier, inc=1, device_id={"ev": y * LINE + beyond[0]}, device_id_type=MESH)
+    peers = 3
     for cond, to in (
         (e < groups - 1, {"ev": e + 1}),
         (e > 0, {"ev": e - 1}),
@@ -87,7 +98,14 @@
             functools.partial(pl.semaphore_signal, barrier, inc=1, device_id=to, device_id_type=MESH)
         )
         peers = peers + cond.astype(jnp.int32)
-    pl.semaphore_wait(barrier, peers)
+    for p in range(pieces - 1):
+        for at, to in (
+            (by_way(p)[0], seam_lo), (seam_hi, by_way(p)[0]), (by_way(p)[1], seam_hi), (seam_lo, by_way(p)[1]),
+        ):
+            pl.when(g == at)(
+                functools.partial(pl.semaphore_signal, barrier, inc=1, device_id={"gx": to}, device_id_type=MESH)
+            )
+            peers = peers + (g == to).astype(jnp.int32)
 
     def term(chunk, side, target):
         p, r0, n = chunk
@@ -145,74 +163,84 @@
         await_recv(part(ym, chunk, 0), ("s+", c))
         await_recv(part(yp, chunk, 1), ("s-", c))
 
-    def unit(c, at, target, slot):
+    def total_of(p, r, lanes):
+        total = own[p, r, :, lanes].astype(f32) + ym[p, r, :, lanes].astype(f32)
+        return total + yp[p, r, :, lanes].astype(f32)
+
+    def lanes_of(target):
+        return pl.ds(pl.multiple_of(target * block, block), block)
+
+    def device_on_line(target):
+        return {"ev": y * LINE + target}
+
+    def pair_stage(c):
         p, r0, n = CHUNKS[c]
-        rightward = target > at
-        first = at == (0 if rightward else LINE - 1)
-        lanes = pl.ds(target * block, block)
         rows = pl.ds(r0, n)
-        name = ("l" if rightward else "r", c, target)
-
-        def landing(source):
-            short = source in (0, LINE - 1) and abs(target - source) > 1
-            if rightward:
-                return left16 if short else left32
-            return right16 if short else right32
-
-        arrived = landing(at - 1 if rightward else at + 1)
-        to = landing(at)
-        staged = line16 if to.dtype == bf16 else line32
-        if not first:
-            await_recv(arrived.at[p, rows, :, lanes], name)
+
+        def via_copy(j):
+            return lambda: via_out.at[j, p, rows], lambda: via.at[j, p, rows], ("via", c, j), device_on_line(mate)
+
+        def first():
+            for j in range(2):
+                lanes = lanes_of(beyond[1 - j])
+
+                def add(t, carry):
+                    r = pl.ds(r0 + 8 * t, 8)
+                    via_out[j, p, r] = total_of(p, r, lanes).astype(bf16)
+                    return carry
+
+                lax.fori_loop(0, n // 8, add, 0)
+                make_copy(*via_copy(j)).start()
+
+        pl.when(at_end)(first)
+        for j in range(2):
+            drains.append((at_end, lambda j=j: make_copy(*via_copy(j)).wait_send()))
+        lanes = lanes_of(mate)
 
         def add(t, carry):
             r = pl.ds(r0 + 8 * t, 8)
-            total = own[p, r, :, lanes].astype(f32) + ym[p, r, :, lanes].astype(f32)
-            total = total + yp[p, r, :, lanes].astype(f32)
-            if not first:
-                total = total + arrived[p, r, :, lanes].astype(f32)
-            staged[p, r, :, lanes] = total.astype(staged.dtype)
+            near_out[p, r] = total_of(p, r, lanes)
             return carry
 
         lax.fori_loop(0, n // 8, add, 0)
-        make = lambda: pltpu.make_async_remote_copy(
-            src_ref=staged.at[p, rows, :, lanes], dst_ref=to.at[p, rows, :, lanes],
-            send_sem=s("linesend", c, slot), recv_sem=s("recv", *name),
-            device_id={"ev": e + 1 if rightward else e - 1}, device_id_type=MESH,
-        )
-        make().start()
-        return lambda: make().wait_send()
-
-    line_drains = {at: [] for at in range(LINE)}
-
-    def line_stage(c, plan):
-        for at, units in plan.items():
-            def run(at=at, units=units):
-                for target, slot in units:
-                    line_drains[at].append(unit(c, at, target, slot))
-            pl.when(z == at)(run)
-
-    hop0 = {0: [(3, 0), (2, 1), (1, 2)], 3: [(0, 0), (1, 1), (2, 2)]}
-    hop1 = {1: [(3, 0), (2, 1)], 2: [(0, 0), (1, 1)]}
-    hop2 = {2: [(3, 2)], 1: [(0, 2)]}
+        send(lambda: near_out.at[p, rows], lambda: near.at[p, rows], ("near", c), device_on_line(mate))
+
+    def far_stage(c):
+        p, r0, n = CHUNKS[c]
+        rows = pl.ds(r0, n)
+
+        def far_copy(j):
+            to = device_on_line(beyond[j])
+            return lambda: far_out.at[j, p, rows], lambda: far.at[p, rows], ("far", c), to, ("far_out", c, j)
+
+        def second():
+            for j in range(2):
+                lanes = lanes_of(beyond[j])
+                await_recv(via.at[j, p, rows], ("via", c, j))
+
+                def add(t, carry):
+                    r = pl.ds(r0 + 8 * t, 8)
+                    far_out[j, p, r] = total_of(p, r, lanes) + via[j, p, r].astype(f32)
+                    return carry
+
+                lax.fori_loop(0, n // 8, add, 0)
+                make_copy(*far_copy(j)).start()
+
+        pl.when(inner)(second)
+        for j in range(2):
+            drains.append((inner, lambda j=j: make_copy(*far_copy(j)).wait_send()))
 
     def finish(c):
         p, r0, n = CHUNKS[c]
         zg = p % per_kernel
         rows = pl.ds(r0, n)
         lanes = pl.ds(pl.multiple_of(z * block, block), block)
-        for at in range(LINE):
-            here = pl.ds(at * block, block)
-            if at > 0:
-                await_recv(left32.at[p, rows, :, here], ("l", c, at), z == at)
-            if at < LINE - 1:
-                await_recv(right32.at[p, rows, :, here], ("r", c, at), z == at)
+        await_recv(near.at[p, rows], ("near", c))
+        await_recv(far.at[p, rows], ("far", c))
 
         def add(t, carry):
             r = pl.ds(r0 + 8 * t, 8)
-            total = own[p, r, :, lanes].astype(f32) + ym[p, r, :, lanes].astype(f32)
-            total = total + yp[p, r, :, lanes].astype(f32)
-            total = total + left32[p, r, :, lanes] + right32[p, r, :, lanes]
+            total = total_of(p, r, lanes) + near[p, r] + far[p, r]
             cells[pl.ds(16 * PLANES * t, 16 * PLANES), :] = (total / ill[zg, r]).reshape(16 * PLANES, block)
             return carry
 
@@ -222,8 +250,27 @@
                 picked = cells[pl.ds(side * PLANES + plane, n, stride=2 * PLANES), :]
                 xe[p, plane, 2 + side, rows, :] = picked.astype(bf16)
         src = lambda: xe.at[p, :, pl.ds(2, 2), rows, :]
-        send(src, lambda: xe.at[p, :, pl.ds(0, 2), rows, :], ("x+", c), {"gx": g + 1}, g < owners - 1)
-        send(src, lambda: xe.at[p, :, pl.ds(4, 2), rows, :], ("x-", c), {"gx": g - 1}, g > 0)
+        direct_up, direct_down = g < owners - 1, g > 0
+        if p < pieces - 1:
+            direct_up, direct_down = direct_up & (g != seam_lo), direct_down & (g != seam_hi)
+            there = lambda: passed.at[:, :, rows, :]
+            for name, source, to in (("u", seam_lo, by_way(p)[0]), ("v", seam_hi, by_way(p)[1])):
+                send(src, there, (name, c), {"gx": jnp.int32(to)}, cond=g == source)
+        send(src, lambda: xe.at[p, :, pl.ds(0, 2), rows, :], ("x+", c), {"gx": g + 1}, cond=direct_up)
+        send(src, lambda: xe.at[p, :, pl.ds(4, 2), rows, :], ("x-", c), {"gx": g - 1}, cond=direct_down)
+
+    def pass_on(c):
+        p, r0, n = CHUNKS[c]
+        if p == pieces - 1:
+            return
+        rows = pl.ds(r0, n)
+        there = lambda: passed.at[:, :, rows, :]
+        for name, at, to, first, arrival in (
+            ("u", by_way(p)[0], seam_hi, 0, "x+"), ("v", by_way(p)[1], seam_lo, 4, "x-"),
+        ):
+            await_recv(there(), (name, c), g == at)
+            dst = lambda first=first: xe.at[p, :, pl.ds(first, 2), rows, :]
+            send(there, dst, (arrival, c), {"gx": jnp.int32(to)}, (name + "on", c), cond=g == at)
 
     def smooth_x(p):
         zg = p % per_kernel
@@ -244,8 +291,8 @@
             be[p, 1, a + 1] = bounded[:, block:]
             two = pl.ds(a, 2)
             src = lambda two=two: be.at[p, 1, two]
-            send(src, lambda two=two: be.at[p, 0, two], ("y+", p, a), {"ev": e + 1}, e < groups - 1)
-            send(src, lambda two=two: be.at[p, 2, two], ("y-", p, a), {"ev": e - 1}, e > 0)
+            send(src, lambda two=two: be.at[p, 0, two], ("y+", p, a), {"ev": e + 1}, cond=e < groups - 1)
+            send(src, lambda two=two: be.at[p, 2, two], ("y-", p, a), {"ev": e - 1}, cond=e > 0)
 
     def smooth_y(p):
         k, zg = p // per_kernel, p % per_kernel
@@ -280,8 +327,6 @@
                 ref[...] = jnp.zeros(ref.shape, ref.dtype)
             return fill
 
-        pl.when(z == 0)(zero(left32.at[:, :, :, pl.ds(0, block)]))
-        pl.when(z == LINE - 1)(zero(right32.at[:, :, :, pl.ds((LINE - 1) * block, block)]))
         pl.when(g == 0)(zero(xe.at[:, :, pl.ds(0, 2)]))
         pl.when(g == owners - 1)(zero(xe.at[:, :, pl.ds(4, 2)]))
         pl.when(e == 0)(zero(be.at[:, 0]))
@@ -296,14 +341,16 @@
                 )
 
     chunks = len(CHUNKS)
-    send_across(0)
-    send_raw(0)
-    send_across(1)
     for c in range(chunks):
         for name, make in loads(c):
             make().start()
     for make in ill_loads():
         make().start()
+    prepare()
+    pl.semaphore_wait(barrier, peers)
+    send_across(0)
+    send_raw(0)
+    send_across(1)
     ready = [max(c for c in range(chunks) if CHUNKS[c][0] == p) + 3 for p in range(pieces)]
     for slot in range(chunks + 4):
         if slot < chunks:
@@ -313,18 +360,17 @@
             if slot + 2 < chunks:
                 send_across(slot + 2)
         if slot == 0:
-            prepare()
             for make in ill_loads():
                 make().wait()
         if 0 <= slot - 1 < chunks:
             ring_done(slot - 1)
-            line_stage(slot - 1, hop0)
-        if 0 <= slot - 2 < chunks:
-            line_stage(slot - 2, hop2)
-        if 0 <= slot - 1 < chunks:
-            line_stage(slot - 1, hop1)
+            pair_stage(slot - 1)
         if 0 <= slot - 2 < chunks:
             finish(slot - 2)
+        if 0 <= slot - 1 < chunks:
+            far_stage(slot - 1)
+        if 0 <= slot - 2 < chunks:
+            pass_on(slot - 2)
         for p in range(pieces):
             if slot == ready[p]:
                 smooth_x(p)
@@ -334,11 +380,6 @@
 
     for cond, drain in drains:
         when(cond, drain)
-    for at, waits in line_drains.items():
-        def run(waits=waits):
-            for wait in waits:
-                wait()
-        pl.when(z == at)(run)
     assert len(index) <= SEMS, len(index)
 
 
@@ -353,17 +394,21 @@
     vmem, smem = pl.BlockSpec(memory_space=pltpu.VMEM), pl.BlockSpec(memory_space=pltpu.SMEM)
     hbm = pl.BlockSpec(memory_space=pl.ANY)
     wide = (pieces, slab // 2, 2 * PLANES, span)
+    unit = (pieces, slab // 2, 2 * PLANES, block)
     out = pl.pallas_call(
         functools.partial(kernel, (owners, groups)),
         out_shape=jax.ShapeDtypeStruct((kernels, planes, slab, block), bf16),
         in_specs=[hbm, hbm, vmem, vmem, smem, smem],
         out_specs=vmem,
-        scratch_shapes=[pltpu.VMEM(wide, bf16)] * 8
-        + [pltpu.VMEM(wide, f32)] * 3
+        scratch_shapes=[pltpu.VMEM(wide, bf16)] * 5
+        + [pltpu.VMEM((2, *unit), bf16)] * 2
+        + [pltpu.VMEM(unit, f32)] * 3
         + [
+            pltpu.VMEM((2, *unit), f32),
             pltpu.VMEM((planes // PLANES, slab // 2, 2 * PLANES, block), f32),
             pltpu.VMEM((slab * PLANES, block), f32),
             pltpu.VMEM((pieces, PLANES, 6, slab // 2, block), bf16),
+            pltpu.VMEM((PLANES, 2, slab // 2, block), bf16),
             pltpu.VMEM((pieces, 3, PLANES, slab, block), bf16),
             pltpu.VMEM((count * slab, slab + 2 * BAND), bf16),
             pltpu.VMEM((block + 2 * BAND, count * block), bf16),

time: 124 us -> 115 us (0.927)
  Pallas kernels: 122 us -> 112 us
    pallas_call x1, Pallas kernels: 122 us -> 112 us  [per_device(): pl.pallas_call(functools.partial(kernel, (owners, groups)), out_shape=jax...]
where the time goes in v3:
time: 115 us
  Pallas kernels  112 us (97%)
  local copies, waits for them, and re-layouts  2.18 us (2%)
    pallas_call x1, Pallas kernels, per_device(): pl.pallas_call(functools.partial(kernel, (owners, groups)), out_shape=jax...  112 us

profile of v3, /device:TPU:15, one launch (start us, length us, event | category | flops | bytes accessed | tf_op | source)
XLA Modules:
  0.0 114.6 jit_solution(12392479212822536418)
XLA Ops:
  0.0 112.4 %condition.1 = bf16[2,8,128,128]{3,2,1,0:T(8,128)(2,1)} custom-call(bf16[128,2,8,2048]{3,2,1,0:T(8,128)(2,1)} %bitcast.3, f32[128,8,128]{2,1,0:T(8,128)} %ill_hbm.1, s32[8,128]{1,0:T(8,128)} %cx_ref.1, s32[8,128]{1,0:T(8,128)} %bitcast.5, f32[3]{0:T(128)} %wx_ref.1, f32[3]{0:T(128)} %wy_ref.1), custom_call_target="tpu_custom_call" | custom-call | flops 2000000000 | bytes 16000000 | tf_op jit(solution)/shard_map/condition/pallas_call | solution.py:398
  112.4 2.2 %copy.7 = bf16[128,2,8,128]{3,2,1,0:T(8,128)(2,1)} copy(bf16[128,2,8,128]{3,0,2,1:T(8,128)(2,1)} %bitcast.4) | data formatting | bytes 1048576 | tf_op jit(solution)/shard_map/transpose | solution.py:424

commit v4 on v3

--- a/solution.py
+++ b/solution.py
@@ -32,7 +32,7 @@
 
 def kernel(
     sizes, x_hbm, ill_hbm, cx_ref, cy_ref, wx_ref, wy_ref, out_ref,
-    own, nxt, got, ym, yp, via, via_out, near, near_out, far, far_out, ill, cells, xe, passed, be, mx, my, cyt, sem,
+    own, nxt, got, ym, yp, via, via_out, near, near_out, far, far_out, late, late_out, ill, cells, xe, passed, be, mx, my, cyt, sem,
 ):
     owners, groups = sizes
     slab, kernels, planes, full_y = x_hbm.shape
@@ -211,6 +211,8 @@
 
         def far_copy(j):
             to = device_on_line(beyond[j])
+            if c == len(CHUNKS) - 1:
+                return lambda: late_out.at[j], lambda: late, ("far", c), to, ("far_out", c, j)
             return lambda: far_out.at[j, p, rows], lambda: far.at[p, rows], ("far", c), to, ("far_out", c, j)
 
         def second():
@@ -220,7 +222,11 @@
 
                 def add(t, carry):
                     r = pl.ds(r0 + 8 * t, 8)
-                    far_out[j, p, r] = total_of(p, r, lanes) + via[j, p, r].astype(f32)
+                    total = total_of(p, r, lanes) + via[j, p, r].astype(f32)
+                    if c == len(CHUNKS) - 1:
+                        late_out[j, pl.ds(8 * t, 8)] = total.astype(bf16)
+                    else:
+                        far_out[j, p, r] = total
                     return carry
 
                 lax.fori_loop(0, n // 8, add, 0)
@@ -236,11 +242,12 @@
         rows = pl.ds(r0, n)
         lanes = pl.ds(pl.multiple_of(z * block, block), block)
         await_recv(near.at[p, rows], ("near", c))
-        await_recv(far.at[p, rows], ("far", c))
+        await_recv(late if c == len(CHUNKS) - 1 else far.at[p, rows], ("far", c))
 
         def add(t, carry):
             r = pl.ds(r0 + 8 * t, 8)
-            total = total_of(p, r, lanes) + near[p, r] + far[p, r]
+            beyond_pair = late[pl.ds(8 * t, 8)].astype(f32) if c == len(CHUNKS) - 1 else far[p, r]
+            total = total_of(p, r, lanes) + near[p, r] + beyond_pair
             cells[pl.ds(16 * PLANES * t, 16 * PLANES), :] = (total / ill[zg, r]).reshape(16 * PLANES, block)
             return carry
 
@@ -351,7 +358,8 @@
     send_across(0)
     send_raw(0)
     send_across(1)
-    ready = [max(c for c in range(chunks) if CHUNKS[c][0] == p) + 3 for p in range(pieces)]
+    last = [max(c for c in range(chunks) if CHUNKS[c][0] == p) for p in range(pieces)]
+    ready = [last[p] + (3, 3, 4, 3)[p] for p in range(pieces)]
     for slot in range(chunks + 4):
         if slot < chunks:
             ring_stage(slot)
@@ -375,7 +383,7 @@
             if slot == ready[p]:
                 smooth_x(p)
         for p in range(pieces):
-            if slot == (ready[-1] if p == pieces - 2 else ready[p] + (1 if p == pieces - 1 else 2)):
+            if slot == ready[-1] + (1 if p == pieces - 1 else 0):
                 smooth_y(p)
 
     for cond, drain in drains:
@@ -405,6 +413,8 @@
         + [pltpu.VMEM(unit, f32)] * 3
         + [
             pltpu.VMEM((2, *unit), f32),
+            pltpu.VMEM((CHUNKS[-1][2], *unit[2:]), bf16),
+            pltpu.VMEM((2, CHUNKS[-1][2], *unit[2:]), bf16),
             pltpu.VMEM((planes // PLANES, slab // 2, 2 * PLANES, block), f32),
             pltpu.VMEM((slab * PLANES, block), f32),
             pltpu.VMEM((pieces, PLANES, 6, slab // 2, block), bf16),

time: 115 us -> 112 us (0.974)
  Pallas kernels: 112 us -> 110 us
    pallas_call x1, Pallas kernels: 112 us -> 110 us  [per_device(): pl.pallas_call(functools.partial(kernel, (owners, groups)), out_shape=jax...]
where the time goes in v4:
time: 112 us
  Pallas kernels  110 us (98%)
  local copies, waits for them, and re-layouts  2.18 us (2%)
    pallas_call x1, Pallas kernels, per_device(): pl.pallas_call(functools.partial(kernel, (owners, groups)), out_shape=jax...  110 us

profile of v4, /device:TPU:15, one launch (start us, length us, event | category | flops | bytes accessed | tf_op | source)
XLA Modules:
  0.0 112.1 jit_solution(9347276977670921223)
XLA Ops:
  0.0 109.9 %condition.1 = bf16[2,8,128,128]{3,2,1,0:T(8,128)(2,1)} custom-call(bf16[128,2,8,2048]{3,2,1,0:T(8,128)(2,1)} %bitcast.3, f32[128,8,128]{2,1,0:T(8,128)} %ill_hbm.1, s32[8,128]{1,0:T(8,128)} %cx_ref.1, s32[8,128]{1,0:T(8,128)} %bitcast.5, f32[3]{0:T(128)} %wx_ref.1, f32[3]{0:T(128)} %wy_ref.1), custom_call_target="tpu_custom_call" | custom-call | flops 2000000000 | bytes 16000000 | tf_op jit(solution)/shard_map/condition/pallas_call | solution.py:406
  109.9 2.2 %copy.7 = bf16[128,2,8,128]{3,2,1,0:T(8,128)(2,1)} copy(bf16[128,2,8,128]{3,0,2,1:T(8,128)(2,1)} %bitcast.4) | data formatting | bytes 1048576 | tf_op jit(solution)/shard_map/transpose | solution.py:434

commit v5 on v4

--- a/solution.py
+++ b/solution.py
@@ -32,7 +32,7 @@
 
 def kernel(
     sizes, x_hbm, ill_hbm, cx_ref, cy_ref, wx_ref, wy_ref, out_ref,
-    own, nxt, got, ym, yp, via, via_out, near, near_out, far, far_out, late, late_out, ill, cells, xe, passed, be, mx, my, cyt, sem,
+    own, nxt, got, ym, yp, via, via_out, near, near_out, far, far_out, late, late_out, ill, cells, xe, passed, be, mx, my, cyt, outs, sem,
 ):
     owners, groups = sizes
     slab, kernels, planes, full_y = x_hbm.shape
@@ -314,7 +314,14 @@
             total = product[:, :block]
             for level in range(1, count):
                 total = jnp.where(labels == level, product[:, level * block : (level + 1) * block], total)
-            out_ref[k, deep] = total.astype(out_ref.dtype).reshape(2, slab, block)
+            for b in range(2):
+                cells[pl.ds(a + b, slab, stride=PLANES), :] = total[b * slab : (b + 1) * slab]
+        outs[p] = cells[...].reshape(slab, PLANES, block).astype(outs.dtype)
+        out_copy(p).start()
+
+    def out_copy(p):
+        k, zg = p // per_kernel, p % per_kernel
+        return pltpu.make_async_copy(outs.at[p], out_ref.at[:, k, pl.ds(zg * PLANES, PLANES), :], s("out", p))
 
     def prepare():
         i = lax.broadcasted_iota(jnp.int32, (slab, slab + 2 * BAND), 0)
@@ -386,6 +393,8 @@
             if slot == ready[-1] + (1 if p == pieces - 1 else 0):
                 smooth_y(p)
 
+    for p in range(pieces):
+        out_copy(p).wait()
     for cond, drain in drains:
         when(cond, drain)
     assert len(index) <= SEMS, len(index)
@@ -403,11 +412,11 @@
     hbm = pl.BlockSpec(memory_space=pl.ANY)
     wide = (pieces, slab // 2, 2 * PLANES, span)
     unit = (pieces, slab // 2, 2 * PLANES, block)
-    out = pl.pallas_call(
+    return pl.pallas_call(
         functools.partial(kernel, (owners, groups)),
-        out_shape=jax.ShapeDtypeStruct((kernels, planes, slab, block), bf16),
+        out_shape=jax.ShapeDtypeStruct((slab, kernels, planes, block), bf16),
         in_specs=[hbm, hbm, vmem, vmem, smem, smem],
-        out_specs=vmem,
+        out_specs=hbm,
         scratch_shapes=[pltpu.VMEM(wide, bf16)] * 5
         + [pltpu.VMEM((2, *unit), bf16)] * 2
         + [pltpu.VMEM(unit, f32)] * 3
@@ -423,6 +432,7 @@
             pltpu.VMEM((count * slab, slab + 2 * BAND), bf16),
             pltpu.VMEM((block + 2 * BAND, count * block), bf16),
             pltpu.VMEM((planes, slab, slab), f32),
+            pltpu.VMEM((pieces, slab, PLANES, block), bf16),
             pltpu.SemaphoreType.DMA((SEMS,)),
         ],
         compiler_params=pltpu.CompilerParams(
@@ -431,7 +441,6 @@
         cost_estimate=pl.CostEstimate(flops=2_000_000_000, bytes_accessed=16_000_000, transcendentals=300_000),
         name="condition",
     )(own_part, illumination, classes_x, classes_y.T, widths_x, widths_y)
-    return out.transpose(2, 0, 1, 3)
 
 
 def solution(mesh):

time: 112 us -> 112 us (level)
    transpose x1 -> x0, local copies, waits for them, and re-layouts: 2.18 us -> none  [per_device(): return out.transpose(2, 0, 1, 3)]
    unnamed x0 -> x1, local copies, waits for them, and re-layouts: none -> 1.87 us
where the time goes in v5:
time: 112 us
  Pallas kernels  110 us (98%)
  local copies, waits for them, and re-layouts  1.87 us (2%)
    pallas_call x1, Pallas kernels, per_device(): pl.pallas_call(functools.partial(kernel, (owners, groups)), out_shape=jax...  110 us

profile of v5, /device:TPU:15, one launch (start us, length us, event | category | flops | bytes accessed | tf_op | source)
XLA Modules:
  0.0 111.7 jit_solution(8833260377464135209)
XLA Ops:
  0.0 109.9 %condition.1 = bf16[128,2,8,128]{3,2,1,0:T(8,128)(2,1)} custom-call(bf16[128,2,8,2048]{3,2,1,0:T(8,128)(2,1)} %bitcast.2, f32[128,8,128]{2,1,0:T(8,128)} %ill_hbm.1, s32[8,128]{1,0:T(8,128)} %cx_ref.1, s32[8,128]{1,0:T(8,128)} %bitcast.3, f32[3]{0:T(128)} %wx_ref.1, f32[3]{0:T(128)} %wy_ref.1), custom_call_target="tpu_custom_call" | custom-call | flops 2000000000 | bytes 16000000 | tf_op jit(solution)/shard_map/condition/pallas_call | solution.py:415
  109.9 1.9 %copy.8 = bf16[128,2,8,128]{3,2,1,0:T(8,128)(2,1)} copy(bf16[128,2,8,128]{3,2,1,0:T(8,128)(2,1)} %condition.1) | data formatting | bytes 1048576
